TPU v7x, 32 devices: a whole 2x2x4 slice. The times are simulated.
32 devices in a mesh: batch: 4 (over z), rows: 8 (over y, x, core).
Axes of the slice: x: 2, y: 2, z: 4, core: 2. Of those that a mesh axis runs over, the one named last changes fastest.
Arguments:
- level_two: bfloat16 [8, 64, 256, 256], P('batch', 'rows'), parts along dimension 0, may hold values from -130 to 130
- level_three: bfloat16 [8, 32, 128, 512], P('batch', 'rows'), parts along dimension 0, may hold values from -130 to 130
- level_four: bfloat16 [8, 16, 64, 1024], P('batch', 'rows'), parts along dimension 0, may hold values from -130 to 130
- level_five: bfloat16 [8, 8, 32, 2048], P('batch', 'rows'), parts along dimension 0, may hold values from -130 to 130
- lateral_two: bfloat16 [256, 256], replicated, may hold values from -0.375 to 0.375
- lateral_three: bfloat16 [512, 256], replicated, may hold values from -0.25 to 0.25
- lateral_four: bfloat16 [1024, 256], replicated, may hold values from -0.1875 to 0.1875
- lateral_five: bfloat16 [2048, 256], replicated, may hold values from -0.125 to 0.125
- lateral_bias: float32 [4, 256], replicated, may hold values from -4 to 4
- smooth_weight: bfloat16 [4, 3, 768, 256], replicated, may hold values from -0.125 to 0.125
- norm_gain: float32 [4, 256], replicated, may hold values from 0.5 to 1.5
- norm_shift: float32 [4, 256], replicated, may hold values from -2 to 2
Outputs:
- pyramid_two: bfloat16 [8, 64, 256, 256], P('batch', 'rows'), parts along dimension 0
- pyramid_three: bfloat16 [8, 32, 128, 256], P('batch', 'rows'), parts along dimension 0
- pyramid_four: bfloat16 [8, 16, 64, 256], P('batch', 'rows'), parts along dimension 0
- pyramid_five: bfloat16 [8, 8, 32, 256], P('batch', 'rows'), parts along dimension 0
There are 4 independent parts, one for each index of `batch`. A program takes and returns all parts, laid end to end along the dimension named above; an argument that names none is the same for every part. Nothing has to cross between parts.
All inputs are finite; a program needn't handle non-finite values.
Results may differ from a plain program's by a relative error of at most 0.0054.
Values may be sent and summed in bfloat16 or wider, within the bound.
A program may use at most 128 MiB of HBM per device.

v0:
```python
import functools

import jax
import jax.numpy as jnp
from jax import lax
from jax.experimental import pallas as pl
from jax.experimental.pallas import tpu as pltpu
from jax.sharding import PartitionSpec as P

GROUPS = 32
EPSILON = 1e-05
F32 = jnp.float32
BF16 = jnp.bfloat16
MESH = pl.DeviceIdType.MESH


def bilinear(cols):
    half = cols // 2
    fine = lax.broadcasted_iota(jnp.int32, (cols, cols), 0)
    coarse = lax.broadcasted_iota(jnp.int32, (cols, cols), 1)
    second = coarse >= half
    coarse = jnp.where(second, coarse - half, coarse)
    near = fine // 2
    odd = fine % 2 == 1
    far = jnp.where(odd, jnp.minimum(near + 1, half - 1), jnp.maximum(near - 1, 0))
    value = jnp.where(coarse == near, 0.75, 0.0) + jnp.where(coarse == far, 0.25, 0.0)
    even_rows = value * jnp.where(second, 0.75, 0.25)
    odd_rows = value * jnp.where(second, 0.25, 0.75)
    return even_rows.astype(BF16), odd_rows.astype(BF16)


def mm(a, b):
    return jnp.dot(a, b, preferred_element_type=F32)


def kernel(n, geom, *refs):
    images, chans = geom["images"], geom["chans"]
    rows, cols = geom["rows"], geom["cols"]
    it = iter(refs)
    take = lambda count: [next(it) for _ in range(count)]
    feat_hbm, lat_hbm = take(4), take(4)
    bias, smooth_hbm, gain, shift = take(4)
    out_hbm = take(4)
    feat, lat_w = take(4), take(4)
    (smooth,) = take(1)
    big, conv, staged, sends, recvs = take(4), take(4), take(4), take(4), take(4)
    lats = [None] + take(3)
    ups = take(3)
    stat_two, stat_rest, got_two, got_rest = take(4)
    in_sem, w_sem, s_sem, out_sem = take(4)
    halo_send, halo_recv, two_send, two_recv, rest_send, rest_recv = take(6)

    me = lax.axis_index("rows")
    first, last = me == 0, me == n - 1

    feat_copy = [pltpu.make_async_copy(feat_hbm[k], feat[k], in_sem.at[k]) for k in range(4)]
    lat_copy = [pltpu.make_async_copy(lat_hbm[k], lat_w[k], w_sem.at[k]) for k in range(4)]
    smooth_copy = [
        pltpu.make_async_copy(smooth_hbm.at[k], smooth.at[k], s_sem.at[k]) for k in range(4)
    ]
    for k in (3, 2, 1, 0):
        lat_copy[k].start()
        feat_copy[k].start()
    for k in (3, 2, 0, 1):
        smooth_copy[k].start()

    barrier = pltpu.get_barrier_semaphore()
    for d in range(1, n):
        pl.semaphore_signal(
            barrier, inc=1, device_id={"rows": lax.rem(me + d, n)}, device_id_type=MESH
        )

    @pl.when(first)
    def _():
        for k in range(4):
            recvs[k][0] = jnp.zeros_like(recvs[k][0])

    @pl.when(last)
    def _():
        for k in range(4):
            recvs[k][1] = jnp.zeros_like(recvs[k][1])

    for k in range(3):
        even, odd = bilinear(cols[k])
        ups[k][0] = even
        ups[k][1] = odd

    def halo_copy(k, way):
        return pltpu.make_async_remote_copy(
            src_ref=sends[k].at[way],
            dst_ref=recvs[k].at[1 - way],
            send_sem=halo_send.at[k, way],
            recv_sem=halo_recv.at[k, 1 - way],
            device_id={"rows": lax.rem(me + (1 if way else n - 1), n)},
            device_id_type=MESH,
        )

    def halo_start(k):
        @pl.when(jnp.logical_not(first))
        def _():
            halo_copy(k, 0).start()

        @pl.when(jnp.logical_not(last))
        def _():
            halo_copy(k, 1).start()

    def halo_wait(k):
        @pl.when(jnp.logical_not(last))
        def _():
            halo_copy(k, 0).wait_recv()

        @pl.when(jnp.logical_not(first))
        def _():
            halo_copy(k, 1).wait_recv()

    def sent_wait(k):
        @pl.when(jnp.logical_not(first))
        def _():
            halo_copy(k, 0).wait_send()

        @pl.when(jnp.logical_not(last))
        def _():
            halo_copy(k, 1).wait_send()

    for k in (3, 2, 1):
        lat_copy[k].wait()
        feat_copy[k].wait()
        for i in range(images):
            flat = feat[k][i].reshape(rows[k] * cols[k], feat[k].shape[-1])
            value = mm(flat, lat_w[k][...]) + bias[k : k + 1, :]
            lats[k][i] = value.reshape(rows[k], cols[k], chans)
            sends[k][0, i] = value[: cols[k]].astype(BF16)
            sends[k][1, i] = value[(rows[k] - 1) * cols[k] :].astype(BF16)
        if k == 3:
            pl.semaphore_wait(barrier, n - 1)
        halo_start(k)
    lat_copy[0].wait()
    feat_copy[0].wait()
    for i in range(images):
        for way, y in ((0, 0), (1, rows[0] - 1)):
            sends[0][way, i] = (mm(feat[0][i, y], lat_w[0][...]) + bias[0:1, :]).astype(BF16)
    halo_start(0)

    def put(k, i, r, value):
        width = cols[k]
        spot = lax.broadcasted_iota(jnp.int32, value.shape, 0)
        before = jnp.where(spot == 0, 0.0, pltpu.roll(value, 1, 0))
        beyond = jnp.where(spot == width - 1, 0.0, pltpu.roll(value, width - 1, 0))
        big[k][i, r, :, 0:chans] = before.astype(BF16)
        big[k][i, r, :, chans : 2 * chans] = value.astype(BF16)
        big[k][i, r, :, 2 * chans :] = beyond.astype(BF16)

    def center(k, i, r):
        return big[k][i, r, :, chans : 2 * chans].astype(F32)

    def doubled(k, i, phase, r):
        pair = big[k + 1][i, pl.ds(r, 2), :, chans : 2 * chans]
        return mm(ups[k][phase], pair.reshape(cols[k], chans))

    for i in range(images):
        for y in range(rows[3]):
            put(3, i, y + 1, lats[3][i, y])
    halo_wait(3)
    for i in range(images):
        put(3, i, 0, jnp.where(first, center(3, i, 1), recvs[3][0, i].astype(F32)))
        put(3, i, rows[3] + 1, jnp.where(last, center(3, i, rows[3]), recvs[3][1, i].astype(F32)))

    def clear(k):
        @pl.when(first)
        def _():
            for i in range(images):
                big[k][i, 0] = jnp.zeros_like(big[k][i, 0])

        @pl.when(last)
        def _():
            for i in range(images):
                big[k][i, rows[k] + 1] = jnp.zeros_like(big[k][i, rows[k] + 1])

    def edges(k):
        for i in range(images):
            above = recvs[k][0, i].astype(F32) + doubled(k, i, 1, 0)
            below = recvs[k][1, i].astype(F32) + doubled(k, i, 0, rows[k] // 2)
            put(k, i, 0, jnp.where(first, center(k, i, 1), above))
            put(k, i, rows[k] + 1, jnp.where(last, center(k, i, rows[k]), below))

    for k in (2, 1):
        for i in range(images):
            for j in range(rows[k] // 2):
                put(k, i, 2 * j + 1, lats[k][i, 2 * j] + doubled(k, i, 0, j))
                put(k, i, 2 * j + 2, lats[k][i, 2 * j + 1] + doubled(k, i, 1, j + 1))
        halo_wait(k)
        edges(k)
        clear(k + 1)

    pairs = rows[0] // 2

    def merge_two(t, carry):
        i, j = t // pairs, t % pairs
        both = mm(feat[0][i, pl.ds(2 * j, 2)].reshape(2 * cols[0], -1), lat_w[0][...])
        both = both + bias[0:1, :]
        put(0, i, 2 * j + 1, both[: cols[0]] + doubled(0, i, 0, j))
        put(0, i, 2 * j + 2, both[cols[0] :] + doubled(0, i, 1, j + 1))
        return carry

    lax.fori_loop(0, images * pairs, merge_two, 0)

    def conv_rows(k, i, y, count):
        total = None
        for a in range(3):
            band = big[k][i, pl.ds(y + a, count)].reshape(count * cols[k], 3 * chans)
            part = mm(band, smooth[k, a])
            total = part if total is None else total + part
        conv[k][i, pl.ds(y, count)] = total.reshape(count, cols[k], chans)
        return jnp.sum(total, 0, keepdims=True), jnp.sum(total * total, 0, keepdims=True)

    stat_rest[...] = jnp.zeros_like(stat_rest)
    stat_two[...] = jnp.zeros_like(stat_two)

    def conv_whole(k):
        smooth_copy[k].wait()
        for i in range(images):
            total, square = conv_rows(k, i, 0, rows[k])
            slot = ((k - 1) * images + i) * 2
            stat_rest[slot : slot + 1, :] = total
            stat_rest[slot + 1 : slot + 2, :] = square

    conv_whole(3)
    conv_whole(2)

    smooth_copy[0].wait()
    inner = (rows[0] - 2) // 2
    for i in range(images):

        def conv_two(t, carry):
            total, square = conv_rows(0, i, 1 + 2 * t, 2)
            return carry[0] + total, carry[1] + square

        zero = jnp.zeros((1, chans), F32)
        total, square = lax.fori_loop(0, inner, conv_two, (zero, zero))
        stat_two[2 * i : 2 * i + 1, :] = total
        stat_two[2 * i + 1 : 2 * i + 2, :] = square
    halo_wait(0)
    edges(0)
    clear(0)
    clear(1)

    def conv_edges(t, carry):
        i, y = t // 2, (t % 2) * (rows[0] - 1)
        total, square = conv_rows(0, i, y, 1)
        stat_two[pl.ds(2 * i, 1), :] += total
        stat_two[pl.ds(2 * i + 1, 1), :] += square
        return carry

    lax.fori_loop(0, images * 2, conv_edges, 0)

    def stat_copies(mine, got, send_sem, recv_sem):
        return [
            pltpu.make_async_remote_copy(
                src_ref=mine,
                dst_ref=got.at[d],
                send_sem=send_sem.at[d],
                recv_sem=recv_sem.at[d],
                device_id={"rows": lax.rem(me + d, n)},
                device_id_type=MESH,
            )
            for d in range(1, n)
        ]

    two_copies = stat_copies(stat_two, got_two, two_send, two_recv)
    for copy in two_copies:
        copy.start()
    conv_whole(1)
    rest_copies = stat_copies(stat_rest, got_rest, rest_send, rest_recv)
    for copy in rest_copies:
        copy.start()

    size = chans // GROUPS
    same = lax.broadcasted_iota(jnp.int32, (chans, chans), 0) // size
    same = same == lax.broadcasted_iota(jnp.int32, (chans, chans), 1) // size
    same = jnp.where(same, 1.0, 0.0).astype(F32)

    def gathered(mine, got):
        total = mine[...]
        for d in range(1, n):
            total = total + got[d]
        return jnp.dot(
            total, same, precision=lax.Precision.HIGHEST, preferred_element_type=F32
        )

    def finish(k, i, total, square):
        entries = float(rows[k] * n * cols[k] * size)
        mean = total / entries
        variance = square / entries - mean * mean
        scale = lax.rsqrt(variance + EPSILON) * gain[k : k + 1, :]
        offset = shift[k : k + 1, :]

        def row(y, carry):
            staged[k][i, y] = ((conv[k][i, y] - mean) * scale + offset).astype(BF16)
            return carry

        lax.fori_loop(0, rows[k], row, 0)
        copy = pltpu.make_async_copy(staged[k].at[i], out_hbm[k].at[i], out_sem.at[k, i])
        copy.start()
        return copy

    out_copies = []
    for copy in two_copies:
        copy.wait_recv()
    sums = gathered(stat_two, got_two)
    for i in range(images):
        out_copies.append(
            finish(0, i, sums[2 * i : 2 * i + 1, :], sums[2 * i + 1 : 2 * i + 2, :])
        )
    for copy in rest_copies:
        copy.wait_recv()
    sums = gathered(stat_rest, got_rest)
    for k in (1, 2, 3):
        for i in range(images):
            slot = ((k - 1) * images + i) * 2
            out_copies.append(
                finish(k, i, sums[slot : slot + 1, :], sums[slot + 1 : slot + 2, :])
            )
    for k in range(4):
        sent_wait(k)
    for copy in two_copies + rest_copies:
        copy.wait_send()
    for copy in out_copies:
        copy.wait()


def per_device(n, *args):
    feats, lat_ws = args[0:4], args[4:8]
    bias, smooth, gain, shift = args[8:12]
    images, chans = feats[0].shape[0], lat_ws[0].shape[1]
    rows = [f.shape[1] for f in feats]
    cols = [f.shape[2] for f in feats]
    geom = {"images": images, "chans": chans, "rows": rows, "cols": cols}
    any_spec = pl.BlockSpec(memory_space=pl.ANY)
    vmem_spec = pl.BlockSpec(memory_space=pltpu.VMEM)
    outs = [jax.ShapeDtypeStruct((images, r, c, chans), BF16) for r, c in zip(rows, cols)]
    dma = pltpu.SemaphoreType.DMA
    rest_rows = -(-(3 * images * 2) // 8) * 8
    two_rows = -(-(images * 2) // 8) * 8
    scratch = (
        [pltpu.VMEM(f.shape, BF16) for f in feats]
        + [pltpu.VMEM(w.shape, BF16) for w in lat_ws]
        + [pltpu.VMEM(smooth.shape, BF16)]
        + [pltpu.VMEM((images, r + 2, c, 3 * chans), BF16) for r, c in zip(rows, cols)]
        + [pltpu.VMEM(o.shape, F32) for o in outs]
        + [pltpu.VMEM(o.shape, BF16) for o in outs]
        + [pltpu.VMEM((2, images, c, chans), BF16) for c in cols]
        + [pltpu.VMEM((2, images, c, chans), BF16) for c in cols]
        + [pltpu.VMEM(o.shape, F32) for o in outs[1:]]
        + [pltpu.VMEM((2, c, c), BF16) for c in cols[:3]]
        + [
            pltpu.VMEM((two_rows, chans), F32),
            pltpu.VMEM((rest_rows, chans), F32),
            pltpu.VMEM((n, two_rows, chans), F32),
            pltpu.VMEM((n, rest_rows, chans), F32),
        ]
        + [dma((4,)), dma((4,)), dma((4,)), dma((4, images))]
        + [dma((4, 2)), dma((4, 2)), dma((n,)), dma((n,)), dma((n,)), dma((n,))]
    )
    return pl.pallas_call(
        functools.partial(kernel, n, geom),
        out_shape=outs,
        in_specs=[any_spec] * 8 + [vmem_spec, any_spec, vmem_spec, vmem_spec],
        out_specs=[any_spec] * 4,
        scratch_shapes=scratch,
        compiler_params=pltpu.CompilerParams(
            collective_id=0, has_side_effects=True, vmem_limit_bytes=60 * 1024 * 1024
        ),
    )(*args)


def solution(mesh):
    strips = P("batch", "rows", None, None)
    run = functools.partial(per_device, mesh.shape["rows"])
    return jax.shard_map(
        lambda *args: tuple(run(*args)),
        mesh=mesh,
        in_specs=(strips,) * 4 + (P(),) * 8,
        out_specs=(strips,) * 4,
        check_vma=False,
    )
```

profile of v0, /device:TPU:0, one launch (start us, length us, event | category | flops | bytes accessed | tf_op | source)
XLA Modules:
  0.0 34.8 jit_solution(1490260652300035344)
XLA Ops:
  0.6 28.9 %shard_map.147 = (bf16[2,8,256,256]{3,2,1,0:T(8,128)(2,1)}, bf16[2,4,128,256]{3,2,1,0:T(8,128)(2,1)}, bf16[2,2,64,256]{3,2,1,0:T(8,128)(2,1)}, bf16[2,1,32,256]{3,2,1,0:T(8,128)(2,1)}) custom-call(bf16[2,8,256,256]{3,2,1,0:T(8,128)(2,1)} %refs_0_.1, bf16[2,4,128,512]{3,2,1,0:T(8,128)(2,1)} %refs_1_.1, bf16[2,2,64,1024]{3,2,1,0:T(8,128)(2,1)} %refs_2_.1, ...), custom_call_target="tpu_custom_call" | custom-call | tf_op jit(solution)/shard_map/pallas_call | solution.py:364
  29.6 0.0 copy-start
  29.6 0.0 copy-start.1
  29.6 0.0 copy-start.2
  29.6 3.2 %copy.20 = bf16[2,8,256,256]{3,2,1,0:T(8,128)(2,1)} copy(bf16[2,8,256,256]{3,2,1,0:T(8,128)(2,1)} %get-tuple-element.8) | data formatting | bytes 4194304
  32.7 0.0 copy-done
  32.7 0.8 %copy.21 = bf16[2,4,128,256]{3,2,1,0:T(8,128)(2,1)} copy(bf16[2,4,128,256]{3,2,1,0:T(8,128)(2,1)S(1)} %copy-done) | data formatting | bytes 1048576
  33.5 0.0 copy-done.1
  33.5 0.7 %copy.22 = bf16[2,2,64,256]{3,2,1,0:T(8,128)(2,1)} copy(bf16[2,2,64,256]{3,2,1,0:T(8,128)(2,1)S(1)} %copy-done.1) | data formatting | bytes 262144
  34.2 0.0 copy-done.2
  34.2 0.6 %copy.23 = bf16[2,1,32,256]{3,2,1,0:T(8,128)(2,1)} copy(bf16[2,1,32,256]{3,2,1,0:T(8,128)(2,1)S(1)} %copy-done.2) | data formatting | bytes 65536
Async XLA Ops:
  29.6 3.2 %copy-start = (bf16[2,4,128,256]{3,2,1,0:T(8,128)(2,1)S(1)}, bf16[2,4,128,256]{3,2,1,0:T(8,128)(2,1)}, u32[]{:S(2)}) copy-start(bf16[2,4,128,256]{3,2,1,0:T(8,128)(2,1)} %get-tuple-element.9) | copy-start | bytes 1572868
  29.6 4.0 %copy-start.1 = (bf16[2,2,64,256]{3,2,1,0:T(8,128)(2,1)S(1)}, bf16[2,2,64,256]{3,2,1,0:T(8,128)(2,1)}, u32[]{:S(2)}) copy-start(bf16[2,2,64,256]{3,2,1,0:T(8,128)(2,1)} %get-tuple-element.10) | copy-start | bytes 393220
  29.6 4.6 %copy-start.2 = (bf16[2,1,32,256]{3,2,1,0:T(8,128)(2,1)S(1)}, bf16[2,1,32,256]{3,2,1,0:T(8,128)(2,1)}, u32[]{:S(2)}) copy-start(bf16[2,1,32,256]{3,2,1,0:T(8,128)(2,1)} %get-tuple-element.11) | copy-start | bytes 98308
where the time goes:
time: 35 us; the launch traced here: 34.8 us
  Pallas kernels  28.9 us (83%)
  local copies, waits for them, and re-layouts  5.23 us (15%)
  between operations  0.67 us (2%)
    pallas_call x1, Pallas kernels, per_device(): pl.pallas_call(functools.partial(kernel, n, geom), out_shape=outs, in_spe...  28.9 us
    unnamed x10, local copies, waits for them, and re-layouts  5.23 us

commit v1 on v0

--- a/solution.py
+++ b/solution.py
@@ -12,6 +12,7 @@
 F32 = jnp.float32
 BF16 = jnp.bfloat16
 MESH = pl.DeviceIdType.MESH
+KERNEL_BYTES = 56 * 1024 * 1024
 
 
 def bilinear(cols):
@@ -39,15 +40,16 @@
     it = iter(refs)
     take = lambda count: [next(it) for _ in range(count)]
     feat_hbm, lat_hbm = take(4), take(4)
-    bias, smooth_hbm, gain, shift = take(4)
-    out_hbm = take(4)
+    bias, smooth_hbm = take(2)
+    conv = take(4)
+    sums_two, sums_rest = take(2)
     feat, lat_w = take(4), take(4)
     (smooth,) = take(1)
-    big, conv, staged, sends, recvs = take(4), take(4), take(4), take(4), take(4)
+    big, sends, recvs = take(4), take(4), take(4)
     lats = [None] + take(3)
     ups = take(3)
     stat_two, stat_rest, got_two, got_rest = take(4)
-    in_sem, w_sem, s_sem, out_sem = take(4)
+    in_sem, w_sem, s_sem = take(3)
     halo_send, halo_recv, two_send, two_recv, rest_send, rest_recv = take(6)
 
     me = lax.axis_index("rows")
@@ -287,6 +289,25 @@
             total, same, precision=lax.Precision.HIGHEST, preferred_element_type=F32
         )
 
+    for copy in two_copies:
+        copy.wait_recv()
+    sums_two[...] = gathered(stat_two, got_two)
+    for copy in rest_copies:
+        copy.wait_recv()
+    sums_rest[...] = gathered(stat_rest, got_rest)
+    for k in range(4):
+        sent_wait(k)
+    for copy in two_copies + rest_copies:
+        copy.wait_send()
+
+
+def finish_kernel(n, geom, *refs):
+    images, chans = geom["images"], geom["chans"]
+    rows, cols = geom["rows"], geom["cols"]
+    conv, (sums_two, sums_rest, gain, shift) = refs[0:4], refs[4:8]
+    out_hbm, staged, out_sem = refs[8:12], refs[12:16], refs[16]
+    size = chans // GROUPS
+
     def finish(k, i, total, square):
         entries = float(rows[k] * n * cols[k] * size)
         mean = total / entries
@@ -304,26 +325,13 @@
         return copy
 
     out_copies = []
-    for copy in two_copies:
-        copy.wait_recv()
-    sums = gathered(stat_two, got_two)
-    for i in range(images):
-        out_copies.append(
-            finish(0, i, sums[2 * i : 2 * i + 1, :], sums[2 * i + 1 : 2 * i + 2, :])
-        )
-    for copy in rest_copies:
-        copy.wait_recv()
-    sums = gathered(stat_rest, got_rest)
-    for k in (1, 2, 3):
+    for k in range(4):
         for i in range(images):
-            slot = ((k - 1) * images + i) * 2
+            sums = sums_rest if k else sums_two
+            slot = (max(k - 1, 0) * images + i) * 2
             out_copies.append(
                 finish(k, i, sums[slot : slot + 1, :], sums[slot + 1 : slot + 2, :])
             )
-    for k in range(4):
-        sent_wait(k)
-    for copy in two_copies + rest_copies:
-        copy.wait_send()
     for copy in out_copies:
         copy.wait()
 
@@ -335,7 +343,7 @@
     rows = [f.shape[1] for f in feats]
     cols = [f.shape[2] for f in feats]
     geom = {"images": images, "chans": chans, "rows": rows, "cols": cols}
-    any_spec = pl.BlockSpec(memory_space=pl.ANY)
+    any_spec = pl.BlockSpec(memory_space=pltpu.HBM)
     vmem_spec = pl.BlockSpec(memory_space=pltpu.VMEM)
     outs = [jax.ShapeDtypeStruct((images, r, c, chans), BF16) for r, c in zip(rows, cols)]
     dma = pltpu.SemaphoreType.DMA
@@ -346,8 +354,6 @@
         + [pltpu.VMEM(w.shape, BF16) for w in lat_ws]
         + [pltpu.VMEM(smooth.shape, BF16)]
         + [pltpu.VMEM((images, r + 2, c, 3 * chans), BF16) for r, c in zip(rows, cols)]
-        + [pltpu.VMEM(o.shape, F32) for o in outs]
-        + [pltpu.VMEM(o.shape, BF16) for o in outs]
         + [pltpu.VMEM((2, images, c, chans), BF16) for c in cols]
         + [pltpu.VMEM((2, images, c, chans), BF16) for c in cols]
         + [pltpu.VMEM(o.shape, F32) for o in outs[1:]]
@@ -358,19 +364,29 @@
             pltpu.VMEM((n, two_rows, chans), F32),
             pltpu.VMEM((n, rest_rows, chans), F32),
         ]
-        + [dma((4,)), dma((4,)), dma((4,)), dma((4, images))]
+        + [dma((4,)), dma((4,)), dma((4,))]
         + [dma((4, 2)), dma((4, 2)), dma((n,)), dma((n,)), dma((n,)), dma((n,))]
     )
-    return pl.pallas_call(
+    held = pl.pallas_call(
         functools.partial(kernel, n, geom),
-        out_shape=outs,
-        in_specs=[any_spec] * 8 + [vmem_spec, any_spec, vmem_spec, vmem_spec],
-        out_specs=[any_spec] * 4,
+        out_shape=[pltpu.VMEM(o.shape, F32) for o in outs]
+        + [pltpu.VMEM((two_rows, chans), F32), pltpu.VMEM((rest_rows, chans), F32)],
+        in_specs=[any_spec] * 8 + [vmem_spec, any_spec],
+        out_specs=[vmem_spec] * 6,
         scratch_shapes=scratch,
         compiler_params=pltpu.CompilerParams(
-            collective_id=0, has_side_effects=True, vmem_limit_bytes=60 * 1024 * 1024
+            collective_id=0, has_side_effects=True, vmem_limit_bytes=KERNEL_BYTES
         ),
-    )(*args)
+    )(*args[:10])
+    held = [pltpu.with_memory_space_constraint(h, pltpu.VMEM) for h in held]
+    return pl.pallas_call(
+        functools.partial(finish_kernel, n, geom),
+        out_shape=outs,
+        in_specs=[vmem_spec] * 8,
+        out_specs=[any_spec] * 4,
+        scratch_shapes=[pltpu.VMEM(o.shape, BF16) for o in outs] + [dma((4, images))],
+        compiler_params=pltpu.CompilerParams(vmem_limit_bytes=16 * 1024 * 1024),
+    )(*held, gain, shift)
 
 
 def solution(mesh):

time: 35 us -> 30.6 us (0.87)
  local copies, waits for them, and re-layouts: 5.23 us -> 0.01 us
  Pallas kernels: 28.9 us -> 29.8 us
    unnamed x10 -> x4, local copies, waits for them, and re-layouts: 5.23 us -> 0.01 us
    pallas_call x1 -> x2, Pallas kernels: 28.9 us -> 29.8 us  [the longest x1 27.9 us: per_device(): pl.pallas_call(functools.partial(kernel, n, geom), out_shape=[pltpu.VMEM(...]
where the time goes in v1:
time: 30.6 us; the launch traced here: 30.5 us
  Pallas kernels  29.8 us (97%)
  between operations  0.68 us (2%)
    pallas_call x1, Pallas kernels, per_device(): pl.pallas_call(functools.partial(kernel, n, geom), out_shape=[pltpu.VMEM(...  27.9 us
    pallas_call x1, Pallas kernels, per_device(): pl.pallas_call(functools.partial(finish_kernel, n, geom), out_shape=outs,...  1.87 us

profile of v1, /device:TPU:0, one launch (start us, length us, event | category | flops | bytes accessed | tf_op | source)
XLA Modules:
  0.0 30.5 jit_solution(11613017372584517115)
XLA Ops:
  0.6 0.0 copy-start.1
  0.6 0.0 copy-start
  0.7 27.9 %shard_map.147 = (f32[2,8,256,256]{3,2,1,0:T(8,128)S(1)}, f32[2,4,128,256]{3,2,1,0:T(8,128)S(1)}, f32[2,2,64,256]{3,2,1,0:T(8,128)S(1)}, f32[2,1,32,256]{3,2,1,0...) custom-call(bf16[2,8,256,256]{3,2,1,0:T(8,128)(2,1)} %refs_0_.1, bf16[2,4,128,512]{3,2,1,0:T(8,128)(2,1)} %refs_1_.1, ...), custom_call_target="tpu_custom_call" | custom-call | tf_op jit(solution)/shard_map/pallas_call | solution.py:370
  28.6 0.0 copy-done.1
  28.6 0.0 copy-done
  28.6 1.9 %shard_map.148 = (bf16[2,8,256,256]{3,2,1,0:T(8,128)(2,1)}, bf16[2,4,128,256]{3,2,1,0:T(8,128)(2,1)}, bf16[2,2,64,256]{3,2,1,0:T(8,128)(2,1)}, bf16[2,1,32,256]{3,2,1,0:T(8,128)(2,1)}) custom-call(f32[2,8,256,256]{3,2,1,0:T(8,128)S(1)} %get-tuple-element.10.refs_0_, f32[2,4,128,256]{3,2,1,0:T(8,128)S(1)} %get-tuple-element.11.refs_1_, ...), custom_call_target="tpu_custom_call" | custom-call | tf_op jit(solution)/shard_map/pallas_call | solution.py:382
Async XLA Ops:
  0.6 27.9 %copy-start.1 = (f32[4,256]{1,0:T(4,128)S(1)}, f32[4,256]{1,0:T(4,128)}, u32[]{:S(2)}) copy-start(f32[4,256]{1,0:T(4,128)} %refs_7_.3) | copy-start | bytes 12292
  0.6 27.9 %copy-start = (f32[4,256]{1,0:T(4,128)S(1)}, f32[4,256]{1,0:T(4,128)}, u32[]{:S(2)}) copy-start(f32[4,256]{1,0:T(4,128)} %refs_6_.3) | copy-start | bytes 12292

commit v2 on v1

--- a/solution.py
+++ b/solution.py
@@ -185,27 +185,6 @@
             put(k, i, 0, jnp.where(first, center(k, i, 1), above))
             put(k, i, rows[k] + 1, jnp.where(last, center(k, i, rows[k]), below))
 
-    for k in (2, 1):
-        for i in range(images):
-            for j in range(rows[k] // 2):
-                put(k, i, 2 * j + 1, lats[k][i, 2 * j] + doubled(k, i, 0, j))
-                put(k, i, 2 * j + 2, lats[k][i, 2 * j + 1] + doubled(k, i, 1, j + 1))
-        halo_wait(k)
-        edges(k)
-        clear(k + 1)
-
-    pairs = rows[0] // 2
-
-    def merge_two(t, carry):
-        i, j = t // pairs, t % pairs
-        both = mm(feat[0][i, pl.ds(2 * j, 2)].reshape(2 * cols[0], -1), lat_w[0][...])
-        both = both + bias[0:1, :]
-        put(0, i, 2 * j + 1, both[: cols[0]] + doubled(0, i, 0, j))
-        put(0, i, 2 * j + 2, both[cols[0] :] + doubled(0, i, 1, j + 1))
-        return carry
-
-    lax.fori_loop(0, images * pairs, merge_two, 0)
-
     def conv_rows(k, i, y, count):
         total = None
         for a in range(3):
@@ -226,34 +205,31 @@
             stat_rest[slot : slot + 1, :] = total
             stat_rest[slot + 1 : slot + 2, :] = square
 
-    conv_whole(3)
+    for k in (2, 1):
+        for i in range(images):
+            for j in range(rows[k] // 2):
+                put(k, i, 2 * j + 1, lats[k][i, 2 * j] + doubled(k, i, 0, j))
+                put(k, i, 2 * j + 2, lats[k][i, 2 * j + 1] + doubled(k, i, 1, j + 1))
+        if k == 1:
+            conv_whole(3)
+        halo_wait(k)
+        edges(k)
+        clear(k + 1)
+
+    pairs = rows[0] // 2
+
+    def merge_two(t, carry):
+        i, j = t // pairs, t % pairs
+        both = mm(feat[0][i, pl.ds(2 * j, 2)].reshape(2 * cols[0], -1), lat_w[0][...])
+        both = both + bias[0:1, :]
+        put(0, i, 2 * j + 1, both[: cols[0]] + doubled(0, i, 0, j))
+        put(0, i, 2 * j + 2, both[cols[0] :] + doubled(0, i, 1, j + 1))
+        return carry
+
+    lax.fori_loop(0, images * pairs, merge_two, 0)
+
+    clear(1)
     conv_whole(2)
-
-    smooth_copy[0].wait()
-    inner = (rows[0] - 2) // 2
-    for i in range(images):
-
-        def conv_two(t, carry):
-            total, square = conv_rows(0, i, 1 + 2 * t, 2)
-            return carry[0] + total, carry[1] + square
-
-        zero = jnp.zeros((1, chans), F32)
-        total, square = lax.fori_loop(0, inner, conv_two, (zero, zero))
-        stat_two[2 * i : 2 * i + 1, :] = total
-        stat_two[2 * i + 1 : 2 * i + 2, :] = square
-    halo_wait(0)
-    edges(0)
-    clear(0)
-    clear(1)
-
-    def conv_edges(t, carry):
-        i, y = t // 2, (t % 2) * (rows[0] - 1)
-        total, square = conv_rows(0, i, y, 1)
-        stat_two[pl.ds(2 * i, 1), :] += total
-        stat_two[pl.ds(2 * i + 1, 1), :] += square
-        return carry
-
-    lax.fori_loop(0, images * 2, conv_edges, 0)
 
     def stat_copies(mine, got, send_sem, recv_sem):
         return [
@@ -268,12 +244,37 @@
             for d in range(1, n)
         ]
 
-    two_copies = stat_copies(stat_two, got_two, two_send, two_recv)
-    for copy in two_copies:
-        copy.start()
+    smooth_copy[0].wait()
+    inner = (rows[0] - 2) // 2
+    for i in range(images):
+
+        def conv_two(t, carry):
+            total, square = conv_rows(0, i, 1 + 2 * t, 2)
+            return carry[0] + total, carry[1] + square
+
+        zero = jnp.zeros((1, chans), F32)
+        total, square = lax.fori_loop(0, inner, conv_two, (zero, zero))
+        stat_two[2 * i : 2 * i + 1, :] = total
+        stat_two[2 * i + 1 : 2 * i + 2, :] = square
     conv_whole(1)
     rest_copies = stat_copies(stat_rest, got_rest, rest_send, rest_recv)
     for copy in rest_copies:
+        copy.start()
+    halo_wait(0)
+    edges(0)
+    clear(0)
+
+    def conv_edges(t, carry):
+        i, y = t // 2, (t % 2) * (rows[0] - 1)
+        total, square = conv_rows(0, i, y, 1)
+        stat_two[pl.ds(2 * i, 1), :] += total
+        stat_two[pl.ds(2 * i + 1, 1), :] += square
+        return carry
+
+    lax.fori_loop(0, images * 2, conv_edges, 0)
+
+    two_copies = stat_copies(stat_two, got_two, two_send, two_recv)
+    for copy in two_copies:
         copy.start()
 
     size = chans // GROUPS
@@ -289,12 +290,12 @@
             total, same, precision=lax.Precision.HIGHEST, preferred_element_type=F32
         )
 
+    for copy in rest_copies:
+        copy.wait_recv()
+    sums_rest[...] = gathered(stat_rest, got_rest)
     for copy in two_copies:
         copy.wait_recv()
     sums_two[...] = gathered(stat_two, got_two)
-    for copy in rest_copies:
-        copy.wait_recv()
-    sums_rest[...] = gathered(stat_rest, got_rest)
     for k in range(4):
         sent_wait(k)
     for copy in two_copies + rest_copies:

time: 30.6 us -> 29.8 us (0.974)
  Pallas kernels: 29.8 us -> 29 us
    pallas_call x1, Pallas kernels: 27.9 us -> 27.1 us  [per_device(): pl.pallas_call(functools.partial(kernel, n, geom), out_shape=[pltpu.VMEM(...]
where the time goes in v2:
time: 29.8 us; the launch traced here: 29.6 us
  Pallas kernels  29 us (97%)
  between operations  0.68 us (2%)
    pallas_call x1, Pallas kernels, per_device(): pl.pallas_call(functools.partial(kernel, n, geom), out_shape=[pltpu.VMEM(...  27.1 us
    pallas_call x1, Pallas kernels, per_device(): pl.pallas_call(functools.partial(finish_kernel, n, geom), out_shape=outs,...  1.87 us

profile of v2, /device:TPU:0, one launch (start us, length us, event | category | flops | bytes accessed | tf_op | source)
XLA Modules:
  0.0 29.6 jit_solution(8448648271962526424)
XLA Ops:
  0.6 0.0 copy-start.1
  0.6 0.0 copy-start
  0.7 27.1 %shard_map.147 = (f32[2,8,256,256]{3,2,1,0:T(8,128)S(1)}, f32[2,4,128,256]{3,2,1,0:T(8,128)S(1)}, f32[2,2,64,256]{3,2,1,0:T(8,128)S(1)}, f32[2,1,32,256]{3,2,1,0...) custom-call(bf16[2,8,256,256]{3,2,1,0:T(8,128)(2,1)} %refs_0_.1, bf16[2,4,128,512]{3,2,1,0:T(8,128)(2,1)} %refs_1_.1, ...), custom_call_target="tpu_custom_call" | custom-call | tf_op jit(solution)/shard_map/pallas_call | solution.py:371
  27.8 0.0 copy-done.1
  27.8 0.0 copy-done
  27.8 1.9 %shard_map.148 = (bf16[2,8,256,256]{3,2,1,0:T(8,128)(2,1)}, bf16[2,4,128,256]{3,2,1,0:T(8,128)(2,1)}, bf16[2,2,64,256]{3,2,1,0:T(8,128)(2,1)}, bf16[2,1,32,256]{3,2,1,0:T(8,128)(2,1)}) custom-call(f32[2,8,256,256]{3,2,1,0:T(8,128)S(1)} %get-tuple-element.10.refs_0_, f32[2,4,128,256]{3,2,1,0:T(8,128)S(1)} %get-tuple-element.11.refs_1_, ...), custom_call_target="tpu_custom_call" | custom-call | tf_op jit(solution)/shard_map/pallas_call | solution.py:383
Async XLA Ops:
  0.6 27.1 %copy-start.1 = (f32[4,256]{1,0:T(4,128)S(1)}, f32[4,256]{1,0:T(4,128)}, u32[]{:S(2)}) copy-start(f32[4,256]{1,0:T(4,128)} %refs_7_.3) | copy-start | bytes 12292
  0.6 27.1 %copy-start = (f32[4,256]{1,0:T(4,128)S(1)}, f32[4,256]{1,0:T(4,128)}, u32[]{:S(2)}) copy-start(f32[4,256]{1,0:T(4,128)} %refs_6_.3) | copy-start | bytes 12292
